TPU v7x, 32 devices: a whole 2x2x4 slice. The times are simulated.
32 devices in a mesh: bank: 4 (over y, x), zero: 8 (over z, core).
Axes of the slice: x: 2, y: 2, z: 4, core: 2. Of those that a mesh axis runs over, the one named last changes fastest.
Arguments:
- master_gate: float32 [64, 2048, 1408], P('bank', 'zero'), may hold values from -0.1875 to 0.1875
- master_up: float32 [64, 2048, 1408], P('bank', 'zero'), may hold values from -0.1875 to 0.1875
- master_down: float32 [64, 1408, 2048], P('bank', None, 'zero'), may hold values from -0.21875 to 0.21875
- router_weight: float32 [2048, 64], P('zero', 'bank'), may hold values from -0.125 to 0.125
- router_gain: float32 [2048], P('zero'), may hold values from 0.25 to 1.75
Outputs:
- final_gate: bfloat16 [64, 2048, 1408], P('bank', None, 'zero')
- final_up: bfloat16 [64, 2048, 1408], P('bank', None, 'zero')
- final_down: bfloat16 [64, 1408, 2048], P('bank', 'zero')
- scale_gate: float32 [64, 1408], P('bank', 'zero')
- scale_up: float32 [64, 1408], P('bank', 'zero')
- scale_down: float32 [64, 1408], P('bank', 'zero')
- serve_router: bfloat16 [2048, 64], replicated
All inputs are finite; a program needn't handle non-finite values. Where the computation divides by a largest or mean magnitude, that divisor is 1e-20 or more.
Results may differ from a plain program's by a relative error of at most 0.001.
Values may be sent and summed in bfloat16 or wider, within the bound.
A program may use at most 256 MiB of HBM per device.

v0:
```python
import jax
import jax.numpy as jnp
from jax import lax
from jax.sharding import PartitionSpec as P


def shards(master_gate, master_up, master_down, router_weight, router_gain):
    scale_gate, scale_up, scale_down = lax.pmax(
        (
            jnp.max(jnp.abs(master_gate), axis=1),
            jnp.max(jnp.abs(master_up), axis=1),
            jnp.max(jnp.abs(master_down), axis=2),
        ),
        "zero",
    )
    narrow_gate, narrow_up, narrow_down = (
        (master_gate / jnp.expand_dims(scale_gate, 1)).astype(jnp.bfloat16),
        (master_up / jnp.expand_dims(scale_up, 1)).astype(jnp.bfloat16),
        (master_down / jnp.expand_dims(scale_down, 2)).astype(jnp.bfloat16),
    )
    final_gate, final_up = (
        lax.all_to_all(narrow_gate, "zero", split_axis=2, concat_axis=1, tiled=True),
        lax.all_to_all(narrow_up, "zero", split_axis=2, concat_axis=1, tiled=True),
    )
    final_down = lax.all_to_all(narrow_down, "zero", split_axis=1, concat_axis=2, tiled=True)
    scale_gate = lax.dynamic_slice_in_dim(
        scale_gate, lax.axis_index("zero") * final_gate.shape[2], final_gate.shape[2], axis=1
    )
    scale_up = lax.dynamic_slice_in_dim(
        scale_up, lax.axis_index("zero") * final_up.shape[2], final_up.shape[2], axis=1
    )
    scale_down = lax.dynamic_slice_in_dim(
        scale_down, lax.axis_index("zero") * final_down.shape[1], final_down.shape[1], axis=1
    )
    part_router = (router_weight * router_gain[:, None]).astype(jnp.bfloat16)
    row_router = lax.all_gather(part_router, "zero", axis=0, tiled=True)
    serve_router = lax.all_gather(row_router, "bank", axis=1, tiled=True)
    return (final_gate, final_up, final_down, scale_gate, scale_up, scale_down, serve_router)


def solution(mesh):
    placed = (
        P("bank", "zero", None),
        P("bank", "zero", None),
        P("bank", None, "zero"),
        P("zero", "bank"),
        P("zero"),
    )
    return jax.shard_map(
        shards,
        mesh=mesh,
        in_specs=placed,
        out_specs=(
            P("bank", None, "zero"),
            P("bank", None, "zero"),
            P("bank", "zero", None),
            P("bank", "zero"),
            P("bank", "zero"),
            P("bank", "zero"),
            P(),
        ),
        check_vma=False,
    )
```

profile of v0, /device:TPU:0, one launch (start us, length us, event | category | flops | bytes accessed | tf_op | source)
XLA Modules:
  0.0 985.2 jit_solution(7565016768209817902)
XLA Ops:
  7.2 10.5 %abs_reduce_fusion = f32[16,1408]{1,0:T(8,128)} fusion(f32[16,1408,256]{2,1,0:T(8,128)} %param.7), kind=kLoop, calls=%fused_computation.2 | loop fusion | flops 11511808 | bytes 23158784 | tf_op jit(solution)/shard_map/reduce_max | solution.py:12
  17.7 10.8 %abs_reduce_fusion.1 = f32[16,1408]{1,0:T(8,128)} fusion(f32[16,256,1408]{2,1,0:T(8,128)} %param.6), kind=kLoop, calls=%fused_computation.4 | loop fusion | flops 11511808 | bytes 23158784 | tf_op jit(solution)/shard_map/reduce_max | solution.py:11
  28.6 2.4 abs_reduce_fusion.2
  31.0 23.7 %copy.24 = f32[16,256,1408]{1,0,2:T(8,128)} copy(f32[16,256,1408]{2,1,0:T(8,128)} %param.5) | data formatting | bytes 46137344 | tf_op args[0]
  54.7 32.5 %all-reduce.3.cloned.1.call-done = (f32[16,1408]{1,0:T(8,128)}, f32[16,1408]{1,0:T(8,128)}, f32[16,1408]{1,0:T(8,128)}) async-done(((f32[16,1408]{1,0:T(8,128)}, f32[16,1408]{1,0:T(8,128)}, f32[16,1408]{1,0:T(8,128)}), (f32[16,1408]{1,0:T(8,128)}, f32[16,1408]{1,0:T(8,128)}, f32[16,1408]{1,0:T(8,128)})) %all-reduce.3.cloned.1.call-update) | async-done | bytes 270352 | tf_op jit(solution)/shard_map/pmax | solution.py:8
  87.2 1.1 copy.23
  88.4 14.2 %divide_convert_fusion.1 = bf16[16,256,1408]{1,0,2:T(8,128)(2,1)} fusion(f32[16,256,1408]{1,0,2:T(8,128)} %copy.24, f32[16,1408]{0,1:T(8,128)S(1)} %copy.23), kind=kLoop, calls=%fused_computation.5 | loop fusion | flops 11534336 | bytes 34693120 | tf_op jit(solution)/shard_map/convert_element_type | solution.py:17
  102.6 5.4 all-to-all-start
  108.0 23.7 %copy.28 = f32[16,256,1408]{1,0,2:T(8,128)} copy(f32[16,256,1408]{2,1,0:T(8,128)} %param.6) | data formatting | bytes 46137344 | tf_op args[1]
  132.0 14.2 %divide_convert_fusion = bf16[16,256,1408]{1,0,2:T(8,128)(2,1)} fusion(f32[16,256,1408]{1,0,2:T(8,128)} %copy.28, f32[16,1408]{0,1:T(8,128)S(1)} %copy.27), kind=kLoop, calls=%fused_computation.3 | loop fusion | flops 11534336 | bytes 34693120 | tf_op jit(solution)/shard_map/convert_element_type | solution.py:18
  146.2 213.1 %all-to-all-done = bf16[16,256,1408]{1,0,2:T(8,128)(2,1)} async-done(((bf16[16,256,1408]{1,0,2:T(8,128)(2,1)}), bf16[16,256,1408]{1,0,2:T(8,128)(2,1)}, u32[]{:S(2)}, u32[]{:S(2)}) %all-to-all-start) | async-done | bytes 11534368 | tf_op jit(solution)/shard_map/all_to_all | solution.py:22
  359.4 5.2 all-to-all-start.1
  364.9 32.6 %fusion = bf16[16,1408,256]{2,0,1:T(8,128)(2,1)} fusion(f32[16,1408,256]{2,1,0:T(8,128)} %param.7, f32[16,1408]{0,1:T(8,128)S(1)} %copy.31), kind=kLoop, calls=%fused_computation.1 | loop fusion | flops 11534336 | bytes 34693120 | tf_op jit(solution)/shard_map/convert_element_type | solution.py:19
  397.5 218.4 %all-to-all-done.1 = bf16[16,256,1408]{1,0,2:T(8,128)(2,1)} async-done(((bf16[16,256,1408]{1,0,2:T(8,128)(2,1)}), bf16[16,256,1408]{1,0,2:T(8,128)(2,1)}, u32[]{:S(2)}, u32[]{:S(2)}) %all-to-all-start.1) | async-done | bytes 11534368 | tf_op jit(solution)/shard_map/all_to_all | solution.py:23
  615.9 5.3 all-to-all-start.2
  621.3 257.3 %all_gather.6 = bf16[2048,16]{0,1:T(8,128)(2,1)S(1)} all-gather(bf16[256,16]{0,1:T(8,128)(2,1)S(1)} %multiply_convert_fusion), channel_id=1, replica_groups=mesh['bank'=4,'zero'=8] {'zero'}, dimensions={0}, use_global_device_ids=true | all-gather | bytes 73728 | tf_op jit(solution)/shard_map/all_gather | solution.py:36
  878.5 9.1 all_gather.7
  887.7 1.4 constant_dynamic-slice_fusion.2
  889.8 11.3 %copy.26 = bf16[16,8,256,176]{2,1,3,0:T(8,128)(2,1)} copy(bf16[16,8,256,176]{2,0,3,1:T(8,128)(2,1)} %bitcast.2) | data formatting | bytes 23068672 | tf_op jit(solution)/shard_map/all_to_all | solution.py:22
  901.1 18.0 %all_to_all.42 = bf16[16,2048,176]{1,2,0:T(8,128)(2,1)} reshape(bf16[16,8,256,176]{2,1,3,0:T(8,128)(2,1)} %copy.26) | data formatting | bytes 23068672 | tf_op jit(solution)/shard_map/all_to_all | solution.py:22
  919.1 11.3 %copy.30 = bf16[16,8,256,176]{2,1,3,0:T(8,128)(2,1)} copy(bf16[16,8,256,176]{2,0,3,1:T(8,128)(2,1)} %bitcast.5) | data formatting | bytes 23068672 | tf_op jit(solution)/shard_map/all_to_all | solution.py:23
  930.4 18.0 %all_to_all.46 = bf16[16,2048,176]{1,2,0:T(8,128)(2,1)} reshape(bf16[16,8,256,176]{2,1,3,0:T(8,128)(2,1)} %copy.30) | data formatting | bytes 23068672 | tf_op jit(solution)/shard_map/all_to_all | solution.py:23
  948.4 11.4 %copy.33 = bf16[16,176,8,256]{3,2,1,0:T(8,128)(2,1)} copy(bf16[16,176,8,256]{3,0,1,2:T(8,128)(2,1)} %bitcast.7) | data formatting | bytes 23068672 | tf_op jit(solution)/shard_map/all_to_all | solution.py:25
  959.7 18.0 %all_to_all.50 = bf16[16,176,2048]{2,1,0:T(8,128)(2,1)} reshape(bf16[16,176,8,256]{3,2,1,0:T(8,128)(2,1)} %copy.33) | data formatting | bytes 23068672 | tf_op jit(solution)/shard_map/all_to_all | solution.py:25
  (29 shorter events, 2.0 us)
Async XLA Ops:
  7.2 80.1 %all-reduce.3.cloned.1.call-start = ((), (), s32[]{:S(2)}) async-start(), calls=%async_computation.3 | async-start | bytes 540672 | tf_op jit(solution)/shard_map/pmax | solution.py:8
  7.2 21.3 %slice-start = ((s8[23068672]{0:T(1024)(128)(4,1)}), s8[4194304]{0:T(1024)(128)(4,1)S(1)}, s32[]{:S(2)}) async-start(s8[23068672]{0:T(1024)(128)(4,1)} %bitcast.19), calls=%async_computation.4 | async-start | bytes 8388608
  7.2 21.3 %slice-start.1 = ((s8[23068672]{0:T(1024)(128)(4,1)}), s8[4194304]{0:T(1024)(128)(4,1)S(1)}, s32[]{:S(2)}) async-start(s8[23068672]{0:T(1024)(128)(4,1)} %bitcast.19), calls=%async_computation.5 | async-start | bytes 8388608
  7.2 21.3 %slice-start.2 = ((s8[23068672]{0:T(1024)(128)(4,1)}), s8[4194304]{0:T(1024)(128)(4,1)S(1)}, s32[]{:S(2)}) async-start(s8[23068672]{0:T(1024)(128)(4,1)} %bitcast.19), calls=%async_computation.6 | async-start | bytes 8388608
  17.7 10.8 %slice-start.3 = ((s8[23068672]{0:T(1024)(128)(4,1)}), s8[4194304]{0:T(1024)(128)(4,1)S(1)}, s32[]{:S(2)}) async-start(s8[23068672]{0:T(1024)(128)(4,1)} %bitcast.19), calls=%async_computation.7 | async-start | bytes 8388608
  17.7 10.8 %slice-start.4 = ((s8[23068672]{0:T(1024)(128)(4,1)}), s8[4194304]{0:T(1024)(128)(4,1)S(1)}, s32[]{:S(2)}) async-start(s8[23068672]{0:T(1024)(128)(4,1)} %bitcast.19), calls=%async_computation.8 | async-start | bytes 8388608
  17.7 10.9 %slice-start.5 = ((s8[23068672]{0:T(1024)(128)(4,1)}), s8[2097152]{0:T(1024)(128)(4,1)S(1)}, s32[]{:S(2)}) async-start(s8[23068672]{0:T(1024)(128)(4,1)} %bitcast.19), calls=%async_computation.9 | async-start | bytes 4194304
  102.6 256.8 %all-to-all-start = ((bf16[16,256,1408]{1,0,2:T(8,128)(2,1)}), bf16[16,256,1408]{1,0,2:T(8,128)(2,1)}, u32[]{:S(2)}, u32[]{:S(2)}) async-start(bf16[16,256,1408]{1,0,2:T(8,128)(2,1)} %divide_convert_fusion.1), calls=%async_computation | async-start | bytes 23068672 | tf_op jit(solution)/shard_map/all_to_all | solution.py:22
  108.0 23.7 %copy-start = (f32[16,1408]{1,0:T(8,128)S(1)}, f32[16,1408]{1,0:T(8,128)}, u32[]{:S(2)}) copy-start(f32[16,1408]{1,0:T(8,128)} %get-tuple-element.8) | copy-start | bytes 270340
  132.0 232.6 %copy-start.1 = (f32[16,1408]{1,0:T(8,128)S(1)}, f32[16,1408]{1,0:T(8,128)}, u32[]{:S(2)}) copy-start(f32[16,1408]{1,0:T(8,128)} %get-tuple-element.9) | copy-start | bytes 270340
  359.4 256.5 %all-to-all-start.1 = ((bf16[16,256,1408]{1,0,2:T(8,128)(2,1)}), bf16[16,256,1408]{1,0,2:T(8,128)(2,1)}, u32[]{:S(2)}, u32[]{:S(2)}) async-start(bf16[16,256,1408]{1,0,2:T(8,128)(2,1)} %divide_convert_fusion), calls=%async_computation.1 | async-start | bytes 23068672 | tf_op jit(solution)/shard_map/all_to_all | solution.py:23
  364.9 256.3 %copy-start.2 = (f32[256,16]{0,1:T(8,128)S(1)}, f32[256,16]{0,1:T(8,128)}, u32[]{:S(2)}) copy-start(f32[256,16]{0,1:T(8,128)} %param.8) | copy-start | bytes 49156
  364.9 256.3 %copy-start.3 = (f32[256]{0:T(256)S(1)}, f32[256]{0:T(256)}, u32[]{:S(2)}) copy-start(f32[256]{0:T(256)} %param.9) | copy-start | bytes 3076
  615.9 332.5 %all-to-all-start.2 = ((bf16[16,1408,256]{2,0,1:T(8,128)(2,1)}), bf16[16,1408,256]{2,0,1:T(8,128)(2,1)}, u32[]{:S(2)}, u32[]{:S(2)}) async-start(bf16[16,1408,256]{2,0,1:T(8,128)(2,1)} %fusion), calls=%async_computation.2 | async-start | bytes 23068672 | tf_op jit(solution)/shard_map/all_to_all | solution.py:25
Sparse Core Ops, SparseCore 0:
  31.1 56.0 all-reduce.2
where the time goes:
time: 988 us; the launch traced here: 985 us
  waiting for transfers between devices  464 us (47%)
  blocking collectives  266 us (27%)
  local copies, waits for them, and re-layouts  140 us (14%)
  other arithmetic  84.8 us (9%)
  starting transfers between devices  16 us (2%)
  between operations  14.2 us (1%)
    all_gather x1, blocking collectives, shards(): row_router = lax.all_gather(part_router, 'zero', axis=0, tiled=True)  257 us
    all_to_all x1, waiting for transfers between devices, shards(): lax.all_to_all(narrow_up, 'zero', split_axis=2, concat_axis=1, tiled=True)  218 us
    all_to_all x1, waiting for transfers between devices, shards(): lax.all_to_all(narrow_gate, 'zero', split_axis=2, concat_axis=1, tiled=True)  213 us
    unnamed x23, local copies, waits for them, and re-layouts  48.2 us
    convert_element_type x1, other arithmetic, shards(): (master_down / jnp.expand_dims(scale_down, 2)).astype(jnp.bfloat16)  32.6 us
    pmax x1, waiting for transfers between devices, shards(): lax.pmax((jnp.max(jnp.abs(master_gate), axis=1), jnp.max(jnp.abs(master_u...  32.5 us
    all_to_all x2, local copies, waits for them, and re-layouts, shards(): lax.all_to_all(narrow_down, 'zero', split_axis=1, concat_axis=2, tiled=True)  29.3 us
    all_to_all x2, local copies, waits for them, and re-layouts, shards(): lax.all_to_all(narrow_gate, 'zero', split_axis=2, concat_axis=1, tiled=True)  29.3 us
  transfers between devices with their start and end apart: 4, of which 3 were waited for; matrix products, arithmetic and copies ran while one was open for 12% of the time, Pallas kernels for 0%

commit v1 on v0

--- a/solution.py
+++ b/solution.py
@@ -1,10 +1,17 @@
+import functools
+
 import jax
 import jax.numpy as jnp
 from jax import lax
+from jax.experimental import pallas as pl
+from jax.experimental.pallas import tpu as pltpu
 from jax.sharding import PartitionSpec as P
 
-
-def shards(master_gate, master_up, master_down, router_weight, router_gain):
+MESH = pl.DeviceIdType.MESH
+LANES = 128
+
+
+def plain_shards(master_gate, master_up, master_down, router_weight, router_gain):
     scale_gate, scale_up, scale_down = lax.pmax(
         (
             jnp.max(jnp.abs(master_gate), axis=1),
@@ -38,6 +45,282 @@
     return (final_gate, final_up, final_down, scale_gate, scale_up, scale_down, serve_router)
 
 
+def exchange_kernel(
+    n, banks, gate, up, down, router, gain,
+    out_gate, out_up, out_down, out_scale, out_router,
+    rowbuf, colbuf, slots, partial, gathered, scale, rt,
+    load_sem, send_sem, local_sem, recv_sem,
+    ex1_send, ex1_recv, ex2_send, ex2_recv,
+    r1_send, r1_recv, r2_send, r2_recv,
+):
+    me = lax.axis_index("zero")
+    bank = lax.axis_index("bank")
+    experts, rows, width = gate.shape
+    piece = width // n
+    share = experts // n
+    nx, ns = rowbuf.shape[0], slots.shape[0]
+    sources, outs = (gate, up, down), (out_gate, out_up, out_down)
+
+    def peer(k):
+        return lax.rem(me + k, n)
+
+    def bank_peer(k):
+        return lax.rem(bank + k, banks)
+
+    barrier = pltpu.get_barrier_semaphore()
+    for k in range(1, n):
+        pl.semaphore_signal(barrier, inc=1, device_id=(bank, peer(k)), device_id_type=MESH)
+    for k in range(1, banks):
+        pl.semaphore_signal(barrier, inc=1, device_id=(bank_peer(k), me), device_id_type=MESH)
+    pl.semaphore_wait(barrier, n - 1 + banks - 1)
+
+    bufs = (rowbuf, rowbuf, colbuf)
+
+    def load(m, e):
+        b = lax.rem(e, nx)
+        return pltpu.make_async_copy(sources[m].at[e], bufs[m].at[b], load_sem.at[m // 2, b])
+
+    def stream(m, lo, hi, body):
+        for i in range(min(nx - 1, hi - lo)):
+            load(m, lo + i).start()
+
+        def step(e, _):
+            @pl.when(e + nx - 1 < hi)
+            def _():
+                load(m, e + nx - 1).start()
+
+            load(m, e).wait()
+            body(e, bufs[m].at[lax.rem(e, nx)])
+            return 0
+
+        lax.fori_loop(lo, hi, step, 0)
+
+    def maxima(m):
+        def body(e, x):
+            if m < 2:
+                partial[m, e] = jnp.max(jnp.abs(x[...]), axis=0, keepdims=True)
+            else:
+                top = jnp.abs(x[:, :LANES])
+                for j in range(1, rows // LANES):
+                    top = jnp.maximum(top, jnp.abs(x[:, j * LANES : (j + 1) * LANES]))
+                partial[m, e] = jnp.max(top.T, axis=0, keepdims=True)
+
+        stream(m, 0, experts, body)
+
+    def ex1(m, k):
+        return pltpu.make_async_remote_copy(
+            src_ref=partial.at[m, pl.ds(peer(k) * share, share)],
+            dst_ref=gathered.at[m, k - 1],
+            send_sem=ex1_send.at[m, k - 1],
+            recv_sem=ex1_recv.at[m, k - 1],
+            device_id=(bank, peer(k)),
+            device_id_type=MESH,
+        )
+
+    def ex2(m, k):
+        mine = scale.at[m, pl.ds(me * share, share)]
+        return pltpu.make_async_remote_copy(
+            src_ref=mine,
+            dst_ref=mine,
+            send_sem=ex2_send.at[m, k - 1],
+            recv_sem=ex2_recv.at[m, k - 1],
+            device_id=(bank, peer(k)),
+            device_id_type=MESH,
+        )
+
+    def ex1_start(m):
+        for k in range(1, n):
+            ex1(m, k).start()
+
+    def ex2_start(m):
+        for k in range(1, n):
+            ex1(m, k).wait()
+        top = partial[m, pl.ds(me * share, share)]
+        for k in range(1, n):
+            top = jnp.maximum(top, gathered[m, k - 1])
+        scale[m, pl.ds(me * share, share)] = top
+        for k in range(1, n):
+            ex2(m, k).start()
+
+    def ex2_wait(m):
+        for k in range(1, n):
+            ex2(m, k).wait()
+
+    def bulk(m, e, s, k):
+        p = peer(k)
+        return pltpu.make_async_remote_copy(
+            src_ref=slots.at[s, pl.ds(pl.multiple_of(p * piece, 16), piece)],
+            dst_ref=outs[m].at[e, :, pl.ds(pl.multiple_of(me * rows, LANES), rows)],
+            send_sem=send_sem.at[s, k - 1],
+            recv_sem=recv_sem.at[m, k - 1],
+            device_id=(bank, p),
+            device_id_type=MESH,
+        )
+
+    def own(m, e, s):
+        return pltpu.make_async_copy(
+            slots.at[s, pl.ds(pl.multiple_of(me * piece, 16), piece)],
+            outs[m].at[e, :, pl.ds(pl.multiple_of(me * rows, LANES), rows)],
+            local_sem.at[s],
+        )
+
+    def free(s):
+        for k in range(1, n):
+            bulk(0, 0, s, k).wait_send()
+        own(0, 0, s).wait()
+
+    def send(m, lo, hi):
+        def body(e, x):
+            g = m * experts + e
+            s = lax.rem(g, ns)
+
+            @pl.when(g >= ns)
+            def _():
+                free(s)
+
+            if m < 2:
+                top = scale[m, e]
+                for j in range(width // LANES):
+                    cut = slice(j * LANES, (j + 1) * LANES)
+                    slots[s, cut, :] = (x[:, cut] / top[:, cut]).T.astype(jnp.bfloat16)
+            else:
+                top = scale[m, e]
+                for j in range(width // LANES):
+                    cut = slice(j * LANES, (j + 1) * LANES)
+                    col = jnp.broadcast_to(top[:, cut], (LANES, LANES)).T
+                    for i in range(rows // LANES):
+                        lane = slice(i * LANES, (i + 1) * LANES)
+                        slots[s, cut, lane] = (x[cut, lane] / col).astype(jnp.bfloat16)
+            for k in range(1, n):
+                bulk(m, e, s, k).start()
+            own(m, e, s).start()
+
+        stream(m, lo, hi, body)
+
+    def r1(k):
+        mine = rt.at[pl.ds(pl.multiple_of(bank * router.shape[0], 16), router.shape[0]), pl.ds(pl.multiple_of(me * rows, LANES), rows)]
+        return pltpu.make_async_remote_copy(
+            src_ref=mine, dst_ref=mine, send_sem=r1_send.at[k - 1], recv_sem=r1_recv.at[k - 1],
+            device_id=(bank, peer(k)), device_id_type=MESH,
+        )
+
+    def r2(k):
+        mine = rt.at[pl.ds(pl.multiple_of(bank * router.shape[0], 16), router.shape[0])]
+        return pltpu.make_async_remote_copy(
+            src_ref=mine, dst_ref=mine, send_sem=r2_send.at[k - 1], recv_sem=r2_recv.at[k - 1],
+            device_id=(bank_peer(k), me), device_id_type=MESH,
+        )
+
+    a = experts // 4
+    maxima(0)
+    ex1_start(0)
+    rt[pl.ds(pl.multiple_of(bank * router.shape[0], 16), router.shape[0]), pl.ds(pl.multiple_of(me * rows, LANES), rows)] = (
+        router[...] * gain[...]
+    ).astype(jnp.bfloat16)
+    ex2_start(0)
+    ex2_wait(0)
+    send(0, 0, a)
+    maxima(1)
+    maxima(2)
+    for m in (1, 2):
+        ex1_start(m)
+    for k in range(1, n):
+        r1(k).start()
+    send(0, a, experts)
+    for m in (1, 2):
+        ex2_start(m)
+    for k in range(1, n):
+        r1(k).wait()
+    for k in range(1, banks):
+        r2(k).start()
+    ex2_wait(1)
+    send(1, 0, experts)
+    ex2_wait(2)
+    send(2, 0, experts)
+    for k in range(1, banks):
+        r2(k).wait()
+    out_scale[...] = scale[...]
+    out_router[...] = rt[...]
+    for s in range(min(ns, 3 * experts)):
+        free(s)
+    for m in range(3):
+        for k in range(1, n):
+            whole = outs[m].at[:, :, pl.ds(0, rows)]
+            pltpu.make_async_copy(whole, whole, recv_sem.at[m, k - 1]).wait()
+
+
+def fused_shards(n, banks, master_gate, master_up, master_down, router_weight, router_gain):
+    experts, rows, width = master_gate.shape
+    piece = width // n
+    columns = router_weight.shape[1]
+    final = jax.ShapeDtypeStruct((experts, piece, n * rows), jnp.bfloat16)
+    hbm, vmem = pl.BlockSpec(memory_space=pl.ANY), pl.BlockSpec(memory_space=pltpu.VMEM)
+    dma = pltpu.SemaphoreType.DMA
+    nx, ns, share = 4, 8, experts // n
+    gate, up, down, scale, router = pl.pallas_call(
+        functools.partial(exchange_kernel, n, banks),
+        out_shape=[
+            final,
+            final,
+            final,
+            jax.ShapeDtypeStruct((3, experts, 1, width), jnp.float32),
+            jax.ShapeDtypeStruct((banks * columns, n * rows), jnp.bfloat16),
+        ],
+        in_specs=[hbm, hbm, hbm, vmem, vmem],
+        out_specs=[hbm, hbm, hbm, vmem, vmem],
+        scratch_shapes=[
+            pltpu.VMEM((nx, rows, width), jnp.float32),
+            pltpu.VMEM((nx, width, rows), jnp.float32),
+            pltpu.VMEM((ns, width, rows), jnp.bfloat16),
+            pltpu.VMEM((3, experts, 1, width), jnp.float32),
+            pltpu.VMEM((3, n - 1, share, 1, width), jnp.float32),
+            pltpu.VMEM((3, experts, 1, width), jnp.float32),
+            pltpu.VMEM((banks * columns, n * rows), jnp.bfloat16),
+            dma((2, nx)),
+            dma((ns, n - 1)),
+            dma((ns,)),
+            dma((3, n - 1)),
+            dma((3, n - 1)),
+            dma((3, n - 1)),
+            dma((3, n - 1)),
+            dma((3, n - 1)),
+            dma((n - 1,)),
+            dma((n - 1,)),
+            dma((banks - 1,)),
+            dma((banks - 1,)),
+        ],
+        compiler_params=pltpu.CompilerParams(
+            collective_id=0, has_side_effects=True, vmem_limit_bytes=48 * 1024 * 1024
+        ),
+    )(master_gate, master_up, master_down, router_weight.T, router_gain[None, :])
+    mine = lax.dynamic_slice_in_dim(
+        scale.reshape(3, experts, width), lax.axis_index("zero") * piece, piece, axis=2
+    )
+    return (
+        jnp.swapaxes(gate, 1, 2),
+        jnp.swapaxes(up, 1, 2),
+        down,
+        mine[0],
+        mine[1],
+        mine[2],
+        router.T,
+    )
+
+
+def shards(n, banks, *arrays):
+    experts, rows, width = arrays[0].shape
+    fits = (
+        experts % n == 0
+        and rows % LANES == 0
+        and width % LANES == 0
+        and width // n % 16 == 0
+        and arrays[3].shape[1] % 16 == 0
+        and n > 1
+        and banks > 1
+    )
+    return fused_shards(n, banks, *arrays) if fits else plain_shards(*arrays)
+
+
 def solution(mesh):
     placed = (
         P("bank", "zero", None),
@@ -47,7 +330,7 @@
         P("zero"),
     )
     return jax.shard_map(
-        shards,
+        functools.partial(shards, mesh.shape["zero"], mesh.shape["bank"]),
         mesh=mesh,
         in_specs=placed,
         out_specs=(

time: 988 us -> 807 us (0.82)
  Pallas kernels: 0 us -> 776 us
  waiting for transfers between devices: 464 us -> 0 us
  blocking collectives: 266 us -> 0 us
  local copies, waits for them, and re-layouts: 140 us -> 27.5 us
  other arithmetic: 84.8 us -> 0.01 us
  starting transfers between devices: 16 us -> 0 us
  between operations: 14.2 us -> 0.67 us
    pallas_call x0 -> x1, Pallas kernels: none -> 776 us  [fused_shards(): pl.pallas_call(functools.partial(exchange_kernel, n, banks), out_shape=[f...]
    all_to_all x3 -> x0, waiting for transfers between devices: 432 us -> none  [the longest x1 218 us: shards(): lax.all_to_all(narrow_up, 'zero', split_axis=2, concat_axis=1, tiled=True)]
    all_gather x2 -> x0, blocking collectives: 266 us -> none  [the longest x1 257 us: shards(): row_router = lax.all_gather(part_router, 'zero', axis=0, tiled=True)]
    all_to_all x6 -> x0, local copies, waits for them, and re-layouts: 87.9 us -> none  [the longest x2 29.3 us: shards(): lax.all_to_all(narrow_down, 'zero', split_axis=1, concat_axis=2, tiled=True)]
    convert_element_type x4 -> x0, other arithmetic: 61.1 us -> none  [the longest x1 32.6 us: shards(): (master_down / jnp.expand_dims(scale_down, 2)).astype(jnp.bfloat16)]
    pmax x1 -> x0, waiting for transfers between devices: 32.5 us -> none  [shards(): lax.pmax((jnp.max(jnp.abs(master_gate), axis=1), jnp.max(jnp.abs(master_u...]
    reduce_max x3 -> x0, other arithmetic: 23.7 us -> none  [the longest x1 10.8 us: shards(): jnp.max(jnp.abs(master_up), axis=1)]
    unnamed x23 -> x18, local copies, waits for them, and re-layouts: 48.2 us -> 27.3 us
  transfers between devices with their start and end apart: 4 -> 0, of which waited for: 3 -> 0; matrix products, arithmetic and copies ran while one was open for 12% -> 0% of each run, Pallas kernels for 0% -> 0%
where the time goes in v1:
time: 807 us; the launch traced here: 804 us
  Pallas kernels  776 us (96%)
  local copies, waits for them, and re-layouts  27.5 us (3%)
    pallas_call x1, Pallas kernels, fused_shards(): pl.pallas_call(functools.partial(exchange_kernel, n, banks), out_shape=[f...  776 us
    unnamed x18, local copies, waits for them, and re-layouts  27.3 us

profile of v1, /device:TPU:0, one launch (start us, length us, event | category | flops | bytes accessed | tf_op | source)
XLA Modules:
  0.0 804.0 jit_solution(14427745798633669488)
XLA Ops:
  0.6 0.0 copy-start
  0.6 0.7 copy-done
  1.4 0.0 copy-start.1
  1.4 0.7 copy-done.1
  2.0 775.8 %shard_map.108 = (bf16[16,176,2048]{2,1,0:T(8,128)(2,1)}, bf16[16,176,2048]{2,1,0:T(8,128)(2,1)}, bf16[16,176,2048]{2,1,0:T(8,128)(2,1)}, f32[3,16,1,1408]{3,2,1,0:T(1,128)S(1)}, bf16[64,2048]{1,0:T(8,128)(2,1)S(1)}) custom-call(f32[16,256,1408]{2,1,0:T(8,128)} %gate.1, f32[16,256,1408]{2,1,0:T(8,128)} %up.1, f32[16,1408,256]{2,1,0:T(8,128)} %down.1, ...), custom_call_target="tpu_custom_call" | custom-call | tf_op jit(solution)/shard_map/pallas_call | solution.py:260
  777.8 0.2 constant_dynamic-slice_fusion.2
  778.0 0.6 copy_bitcast_fusion
  778.6 0.6 copy.18
  779.3 0.0 copy-start.2
  779.3 0.0 slice-start
  779.3 0.0 slice-start.1
  779.3 12.0 %copy.23 = bf16[16,2048,176]{1,2,0:T(8,128)(2,1)} copy(bf16[16,2048,176]{1,2,0:T(8,128)(2,1)} %bitcast.18) | data formatting | bytes 23068672
  791.3 0.0 copy-done.2
  791.3 0.0 slice-start.2
  791.3 5.8 copy.24
  797.1 0.0 slice-done
  797.1 0.0 slice-done.1
  797.1 1.7 slice-done.2
  798.9 4.4 copy.25
  803.3 0.7 copy.26
  (1 shorter events, 0.0 us)
Async XLA Ops:
  0.6 0.7 copy-start
  1.4 0.7 copy-start.1
  779.3 12.0 %copy-start.2 = (bf16[16,176,2048]{2,1,0:T(8,128)(2,1)S(1)}, bf16[16,176,2048]{2,1,0:T(8,128)(2,1)}, u32[]{:S(2)}) copy-start(bf16[16,176,2048]{2,1,0:T(8,128)(2,1)} %get-tuple-element.13) | copy-start | bytes 34603012
  779.3 17.8 %slice-start = ((s8[11534336]{0:T(1024)(128)(4,1)}), s8[4194304]{0:T(1024)(128)(4,1)S(1)}, s32[]{:S(2)}) async-start(s8[11534336]{0:T(1024)(128)(4,1)} %bitcast.15), calls=%async_computation | async-start | bytes 8388608
  779.3 17.8 %slice-start.1 = ((s8[11534336]{0:T(1024)(128)(4,1)}), s8[4194304]{0:T(1024)(128)(4,1)S(1)}, s32[]{:S(2)}) async-start(s8[11534336]{0:T(1024)(128)(4,1)} %bitcast.15), calls=%async_computation.1 | async-start | bytes 8388608
  791.3 7.6 slice-start.2
